TPU v7x, 256 devices: a 8x8x2 block of a 8x8x16 slice. The times are simulated.
256 devices in a mesh: group: 2 (over z), dp: 16 (over y, core), tensor: 8 (over x).
Axes of the slice: x: 8, y: 8, z: 2, core: 2. Of those that a mesh axis runs over, the one named last changes fastest.
The devices are a block of a 8x8x16 slice.
Arguments:
- tokens: bfloat16 [4096, 5120], P(('group', 'dp'), 'tensor'), parts along dimension 0, may hold values from -6 to 6
- router: bfloat16 [5120, 8], replicated, may hold values from -0.078125 to 0.078125
- expert_gate: bfloat16 [5120, 32768], P(None, ('dp', 'tensor')), may hold values from -0.078125 to 0.078125
- expert_up: bfloat16 [5120, 32768], P(None, ('dp', 'tensor')), may hold values from -0.078125 to 0.078125
- expert_down: bfloat16 [32768, 5120], P(('dp', 'tensor')), may hold values from -0.09375 to 0.09375
- shared_gate: bfloat16 [5120, 4096], P('dp', 'tensor'), may hold values from -0.078125 to 0.078125
- shared_up: bfloat16 [5120, 4096], P('dp', 'tensor'), may hold values from -0.078125 to 0.078125
- shared_down: bfloat16 [4096, 5120], P('tensor', 'dp'), may hold values from -0.09375 to 0.09375
- expert_ids: int32 [4096], P(('group', 'dp')), parts along dimension 0, may hold values from 0 to 7, as said below
- expert_slots: int32 [4096], P(('group', 'dp')), parts along dimension 0, may hold values from 0 to 31, as said below
Outputs:
- mixed: bfloat16 [4096, 5120], P(('group', 'dp'), 'tensor'), parts along dimension 0
There are 2 independent parts, one for each index of `group`. A program takes and returns all parts, laid end to end along the dimension named above; an argument that names none is the same for every part. Nothing has to cross between parts.
Inputs may be any that keep to these rules, and one draw needn't show every extreme that they name: `expert_ids`: among the tokens of one index of dp no expert has more than 32; in every draw one expert has exactly 32 tokens from every index of dp. `expert_slots`: tokens of one index of dp with the same expert have distinct slots.
All inputs are finite; a program needn't handle non-finite values.
Results may differ from a plain program's by a relative error of at most 0.015.
Values may be sent and summed in bfloat16 or wider, within the bound.
No kernel may reach another device: no remote copies, remote signals or barrier semaphores. Data moves between devices by JAX's collectives and lax.ppermute only.
A program may use at most 128 MiB of HBM per device.

v0:
```python
import jax
import jax.numpy as jnp
from jax import lax
from jax.sharding import PartitionSpec as P


def joined_along(tiles, dim):
    dims = list(tiles.shape[1:])
    dims[dim] *= tiles.shape[0]
    return jnp.moveaxis(tiles, 0, dim).reshape(dims)


def copy_for_each(value, axis):
    copies = jnp.broadcast_to(value, (lax.axis_size(axis), *value.shape))
    return lax.all_to_all(copies, axis, split_axis=0, concat_axis=0, tiled=True)


def gather_directly(value, axis, dim):
    return joined_along(copy_for_each(value, axis), dim)


def side_by_side(arrays, axis, dim, along):
    both = jnp.concatenate(arrays, axis=along)
    out, at, finished = (lax.all_gather(both, axis, axis=dim, tiled=True), 0, [])
    for a in arrays:
        finished.append(lax.slice_in_dim(out, at, at + a.shape[along], axis=along))
        at += a.shape[along]
    return tuple(finished)


def split_up(value, dim, devices):
    before, after = (value.shape[:dim], value.shape[dim + 1 :])
    return jnp.moveaxis(value.reshape(*before, devices, -1, *after), dim, 0)


def sum_at_owner(value, axis, dim):
    tiles = split_up(value, dim, lax.axis_size(axis))
    arrived = lax.all_to_all(tiles, axis, split_axis=0, concat_axis=0, tiled=True)
    return arrived.astype(jnp.float32).sum(axis=0)


def swapped(value, axis, bit):
    mask = 2**bit
    pairs = [(source, source ^ mask) for source in range(lax.axis_size(axis))]
    return lax.ppermute(value, axis, pairs)


def on_device(
    tokens,
    router,
    expert_gate,
    expert_up,
    expert_down,
    shared_gate,
    shared_up,
    shared_down,
    expert_ids,
    expert_slots,
):
    tok_rows, part_width = tokens.shape
    dp_count = lax.axis_size("dp")
    experts = dp_count // 2
    capacity = min(2 * tok_rows // experts, tok_rows // 2)
    gathered = gather_directly(tokens, "tensor", 1)
    logits = jnp.dot(gathered, router, preferred_element_type=jnp.float32)
    one_hot = (expert_ids[:, None] == jnp.arange(experts, dtype=jnp.int32)[None, :]).astype(
        jnp.float32
    )
    gating = jax.nn.sigmoid(jnp.sum(logits * one_hot, axis=1))
    routed = (tokens.astype(jnp.float32) * gating[:, None]).astype(jnp.bfloat16)
    outgoing = (
        jnp.zeros((experts, capacity, part_width), jnp.bfloat16)
        .at[expert_ids, expert_slots]
        .set(routed)
    )
    pieces = side_by_side((shared_gate, shared_up), "dp", 0, 1)
    gate_sum = jnp.dot(gathered, pieces[0], preferred_element_type=jnp.float32)
    up_sum = jnp.dot(gathered, pieces[1], preferred_element_type=jnp.float32)
    shared_hidden = (jax.nn.silu(gate_sum) * up_sum).astype(jnp.bfloat16)
    shared_terms = jnp.dot(
        shared_hidden,
        lax.all_gather(shared_down, "dp", axis=1, tiled=True),
        preferred_element_type=jnp.float32,
    )
    shared_out = lax.psum_scatter(
        shared_terms.astype(jnp.bfloat16), "tensor", scatter_dimension=1, tiled=True
    ).astype(jnp.float32)
    half_cap = capacity // 2
    to_send = outgoing.reshape(dp_count, half_cap, part_width)
    own_half = lax.all_to_all(to_send, "dp", split_axis=0, concat_axis=0, tiled=True)
    partner = swapped(own_half, "dp", 0)
    parity = lax.axis_index("dp") % 2
    odd_host = parity == 1
    lower_half = jnp.where(odd_host, partner, own_half)
    upper_half = jnp.where(odd_host, own_half, partner)
    received = jnp.concatenate([lower_half, upper_half], axis=1)
    source_count = received.shape[0]
    slot_count = received.shape[1]
    slot_total = source_count * slot_count
    portion = lax.all_gather(received, "tensor", axis=2, tiled=True)
    flattened = portion.reshape(slot_total, portion.shape[2])
    gate_e = jnp.dot(flattened, expert_gate, preferred_element_type=jnp.float32)
    up_e = jnp.dot(flattened, expert_up, preferred_element_type=jnp.float32)
    hidden_e = (jax.nn.silu(gate_e) * up_e).astype(jnp.bfloat16)
    expert_terms = jnp.dot(hidden_e, expert_down, preferred_element_type=jnp.float32)
    expert_terms = expert_terms.reshape(source_count, slot_count, expert_terms.shape[1])
    partials = sum_at_owner(expert_terms.astype(jnp.bfloat16), "tensor", 2)
    partner_sum = swapped(partials.astype(jnp.bfloat16), "dp", 0).astype(partials.dtype)
    paired = partials + partner_sum
    kept_half = lax.dynamic_slice_in_dim(paired, parity * half_cap, half_cap, 1).astype(
        jnp.bfloat16
    )
    returned_raw = lax.all_to_all(kept_half, "dp", split_axis=0, concat_axis=0, tiled=True)
    returned = returned_raw.reshape(experts, capacity, part_width)
    expert_out = returned[expert_ids, expert_slots]
    return (shared_out + expert_out.astype(jnp.float32)).astype(jnp.bfloat16)


def solution(mesh):
    in_specs = (
        P(("group", "dp"), "tensor"),
        P(),
        P(None, ("dp", "tensor")),
        P(None, ("dp", "tensor")),
        P(("dp", "tensor"), None),
        P("dp", "tensor"),
        P("dp", "tensor"),
        P("tensor", "dp"),
        P(("group", "dp")),
        P(("group", "dp")),
    )
    out_specs = P(("group", "dp"), "tensor")
    return jax.shard_map(
        on_device, mesh=mesh, in_specs=in_specs, out_specs=out_specs, check_vma=False
    )
```

profile of v0, /device:TPU:515, one launch (start us, length us, event | category | flops | bytes accessed | tf_op | source)
XLA Modules:
  0.0 342.5 jit_solution(5509344661017308061)
XLA Ops:
  6.6 1.2 copy.12
  7.8 1.3 broadcast_in_dim.8
  9.0 7.2 %all-to-all-start = ((bf16[8,128,640]{1,2,0:T(8,128)(2,1)}), bf16[8,128,640]{1,2,0:T(8,128)(2,1)}, u32[]{:S(2)}, u32[]{:S(2)}) async-start(bf16[8,128,640]{1,2,0:T(8,128)(2,1)} %broadcast_in_dim.8), calls=%async_computation | async-start | bytes 2621440 | tf_op jit(solution)/shard_map/all_to_all | solution.py:15
  16.2 19.5 %all-to-all-done = bf16[8,128,640]{1,2,0:T(8,128)(2,1)} async-done(((bf16[8,128,640]{1,2,0:T(8,128)(2,1)}), bf16[8,128,640]{1,2,0:T(8,128)(2,1)}, u32[]{:S(2)}, u32[]{:S(2)}) %all-to-all-start) | async-done | bytes 1310752 | tf_op jit(solution)/shard_map/all_to_all | solution.py:15
  35.7 1.6 fusion.17
  37.5 8.0 %scatter_fusion = bf16[8,32,640]{2,1,0:T(8,128)(2,1)S(1)} fusion(bf16[8,32,640]{2,1,0:T(8,128)(2,1)S(1)} %broadcast_in_dim.18, s32[128]{0:T(128)S(1)} %get-tuple-element.8, bf16[128,640]{1,0:T(8,128)(2,1)S(1)} %multiply_convert_fusion), kind=kCustom, calls=%fused_computation.1 | custom fusion | bytes 492544 | tf_op jit(solution)/shard_map/scatter | solution.py:74
  45.5 40.7 %all_to_all.20 = bf16[16,16,640]{2,1,0:T(8,128)(2,1)S(1)} all-to-all(bf16[16,16,640]{2,1,0:T(8,128)(2,1)S(1)} %bitcast.60), channel_id=1, replica_groups=mesh['group'=2,'dp'=16,'tensor'=8] {'dp'}, dimensions={0} | all-to-all | bytes 655360 | tf_op jit(solution)/shard_map/all_to_all | solution.py:90
  86.2 1.6 collective-permute-done
  87.9 0.9 pad_maximum_fusion.1
  88.9 2.0 pad_maximum_fusion
  91.0 0.7 all-gather.6.cloned.1.call-update
  91.7 63.9 %all-gather.8.cloned.1.call-done = bf16[16,32,5120]{2,1,0:T(8,128)(2,1)} async-done(((bf16[16,32,640]{2,1,0:T(8,128)(2,1)}), bf16[16,32,5120]{2,1,0:T(8,128)(2,1)}) %all-gather.8.cloned.1.call-update) | async-done | bytes 5242896 | tf_op jit(solution)/shard_map/all_gather | solution.py:100
  155.6 4.8 %fusion.40 = f32[512,256]{1,0:T(8,128)S(1)} fusion(bf16[512,5120]{1,0:T(8,128)(2,1)} %bitcast.65, bf16[5120,256]{1,0:T(8,128)(2,1)} %param.12), kind=kOutput, calls=%fused_computation.52 | convolution fusion | flops 1342177280 | bytes 8388608 | tf_op jit(solution)/shard_map/dot_general | solution.py:102
  160.5 11.2 %convolution_convert_fusion = bf16[512,5120]{1,0:T(8,128)(2,1)} fusion(bf16[256,5120]{1,0:T(8,128)(2,1)S(1)} %copy-done, bf16[512,5120]{1,0:T(8,128)(2,1)} %bitcast.66, bf16[5120,256]{1,0:T(8,128)(2,1)} %param.13, f32[512,256]{1,0:T(8,128)S(1)} %fusion.40), kind=kOutput, calls=%fused_computation.3 | convolution fusion | flops 2687762432 | bytes 16252928 | tf_op jit(solution)/shard_map/dot_general | solution.py:105
  171.7 3.7 %copy.16 = bf16[64,8,8,640]{3,2,1,0:T(8,128)(2,1)S(1)} copy(bf16[64,8,8,640]{3,1,2,0:T(8,128)(2,1)} %bitcast.62) | data formatting | bytes 10485760
  175.3 3.1 copy.18
  178.4 6.2 %all-to-all-start.2 = ((bf16[8,16,32,640]{3,2,1,0:T(8,128)(2,1)}), bf16[8,16,32,640]{3,2,1,0:T(8,128)(2,1)}, u32[]{:S(2)}, u32[]{:S(2)}) async-start(bf16[8,16,32,640]{3,2,1,0:T(8,128)(2,1)} %bitcast.58), calls=%async_computation.2 | async-start | bytes 10485760 | tf_op jit(solution)/shard_map/all_to_all | solution.py:38
  184.6 41.0 %all-gather.4.cloned.1.call-done = bf16[5120,1024]{1,0:T(8,128)(2,1)} async-done(((bf16[320,1024]{1,0:T(8,128)(2,1)}), bf16[5120,1024]{1,0:T(8,128)(2,1)}) %all-gather.4.cloned.1.call-update) | async-done | bytes 10485776 | tf_op jit(solution)/shard_map/all_gather | solution.py:24
  225.6 4.4 %fusion.5 = f32[128,512]{0,1:T(8,128)S(1)} fusion(bf16[128,5120]{0,1:T(8,128)(2,1)} %bitcast.1, bf16[5120,1024]{1,0:T(8,128)(2,1)} %all-gather.4.cloned.1.call-done), kind=kOutput, calls=%fused_computation.12 | convolution fusion | flops 671088640 | bytes 6815744 | tf_op jit(solution)/shard_map/dot_general | solution.py:77
  230.1 40.7 %all-gather.6.cloned.1.call-done = bf16[512,5120]{0,1:T(8,128)(2,1)} async-done(((bf16[512,320]{0,1:T(8,128)(2,1)}), bf16[512,5120]{0,1:T(8,128)(2,1)}) %all-gather.6.cloned.1.call-update) | async-done | bytes 5242896 | tf_op jit(solution)/shard_map/all_gather | solution.py:82
  270.7 11.2 %convolution_convert_fusion.1 = bf16[128,5120]{1,0:T(8,128)(2,1)} fusion(bf16[512,5120]{0,1:T(8,128)(2,1)} %all-gather.6.cloned.1.call-done, bf16[128,5120]{0,1:T(8,128)(2,1)} %bitcast.1, bf16[5120,1024]{1,0:T(8,128)(2,1)} %all-gather.4.cloned.1.call-done, f32[128,512]{0,1:T(8,128)S(1)} %fusion.5), kind=kOutput, calls=%fused_computation.4 | convolution fusion | flops 1343225856 | bytes 13369344 | tf_op jit(solution)/shard_map/dot_general | solution.py:80
  281.9 2.4 copy.14
  284.4 17.9 %all-to-all-done.2 = bf16[8,16,32,640]{3,2,1,0:T(8,128)(2,1)} async-done(((bf16[8,16,32,640]{3,2,1,0:T(8,128)(2,1)}), bf16[8,16,32,640]{3,2,1,0:T(8,128)(2,1)}, u32[]{:S(2)}, u32[]{:S(2)}) %all-to-all-start.2) | async-done | bytes 5242912 | tf_op jit(solution)/shard_map/all_to_all | solution.py:38
  302.4 3.4 %convert_reduce_fusion = f32[16,32,640]{2,1,0:T(8,128)S(1)} fusion(bf16[8,16,32,640]{3,2,1,0:T(8,128)(2,1)} %all-to-all-done.2), kind=kLoop, calls=%fused_computation.2 | loop fusion | flops 4915200 | bytes 6553600 | tf_op jit(solution)/shard_map/reduce_sum | solution.py:39
  305.8 1.1 copy-done.1
  307.0 2.7 collective-permute-start.1
  309.7 1.9 collective-permute-done.1
  311.5 2.0 fusion.20
  313.5 7.4 %all-to-all-start.3 = ((bf16[16,16,640]{2,1,0:T(8,128)(2,1)}), bf16[16,16,640]{2,1,0:T(8,128)(2,1)S(1)}, u32[]{:S(2)}, u32[]{:S(2)}) async-start(bf16[16,16,640]{2,1,0:T(8,128)(2,1)} %fusion.20), calls=%async_computation.3 | async-start | bytes 655360 | tf_op jit(solution)/shard_map/all_to_all | solution.py:113
  320.9 1.1 copy.15
  322.0 11.9 %all-to-all-done.3 = bf16[16,16,640]{2,1,0:T(8,128)(2,1)S(1)} async-done(((bf16[16,16,640]{2,1,0:T(8,128)(2,1)}), bf16[16,16,640]{2,1,0:T(8,128)(2,1)S(1)}, u32[]{:S(2)}, u32[]{:S(2)}) %all-to-all-start.3) | async-done | bytes 327712 | tf_op jit(solution)/shard_map/all_to_all | solution.py:113
  333.9 1.4 gather_fusion
  (27 shorter events, 1.3 us)
Async XLA Ops:
  6.5 153.9 %copy-start = (bf16[256,5120]{1,0:T(8,128)(2,1)S(1)}, bf16[256,5120]{1,0:T(8,128)(2,1)}, u32[]{:S(2)}) copy-start(bf16[256,5120]{1,0:T(8,128)(2,1)} %param.14) | copy-start | bytes 7864324
  6.6 9.7 %copy-start.4 = (s32[128]{0:T(128)S(1)}, s32[128]{0:T(128)}, u32[]{:S(2)}) copy-start(s32[128]{0:T(128)} %param.18) | copy-start | bytes 1540
  6.6 9.7 %copy-start.5 = (s32[128]{0:T(128)S(1)}, s32[128]{0:T(128)}, u32[]{:S(2)}) copy-start(s32[128]{0:T(128)} %param.19) | copy-start | bytes 1540
  6.6 29.1 %copy-start.3 = (bf16[5120,8]{0,1:T(8,128)(2,1)S(1)}, bf16[5120,8]{0,1:T(8,128)(2,1)}, u32[]{:S(2)}) copy-start(bf16[5120,8]{0,1:T(8,128)(2,1)} %param.11) | copy-start | bytes 245764
  7.8 29.5 %copy-start.2 = (bf16[128,640]{1,0:T(8,128)(2,1)S(1)}, bf16[128,640]{1,0:T(8,128)(2,1)}, u32[]{:S(2)}) copy-start(bf16[128,640]{1,0:T(8,128)(2,1)} %param.10) | copy-start | bytes 491524
  9.0 26.6 %all-to-all-start = ((bf16[8,128,640]{1,2,0:T(8,128)(2,1)}), bf16[8,128,640]{1,2,0:T(8,128)(2,1)}, u32[]{:S(2)}, u32[]{:S(2)}) async-start(bf16[8,128,640]{1,2,0:T(8,128)(2,1)} %broadcast_in_dim.8), calls=%async_computation | async-start | bytes 2621440 | tf_op jit(solution)/shard_map/all_to_all | solution.py:15
  16.2 139.4 %all-gather.8.cloned.1.call-start = ((), (), s32[]{:S(2)}) async-start(), calls=%async_computation.7 | async-start | bytes 5898240 | tf_op jit(solution)/shard_map/all_gather | solution.py:100
  86.2 1.6 collective-permute-start
  88.8 136.8 %all-gather.4.cloned.1.call-start = ((), (), s32[]{:S(2)}) async-start(), calls=%async_computation.5 | async-start | bytes 11141120 | tf_op jit(solution)/shard_map/all_gather | solution.py:24
  90.9 179.8 %all-gather.6.cloned.1.call-start = ((), (), s32[]{:S(2)}) async-start(), calls=%async_computation.6 | async-start | bytes 5570560 | tf_op jit(solution)/shard_map/all_gather | solution.py:82
  178.4 124.0 %all-to-all-start.2 = ((bf16[8,16,32,640]{3,2,1,0:T(8,128)(2,1)}), bf16[8,16,32,640]{3,2,1,0:T(8,128)(2,1)}, u32[]{:S(2)}, u32[]{:S(2)}) async-start(bf16[8,16,32,640]{3,2,1,0:T(8,128)(2,1)} %bitcast.58), calls=%async_computation.2 | async-start | bytes 10485760 | tf_op jit(solution)/shard_map/all_to_all | solution.py:38
  184.6 136.3 %reduce-scatter.4.cloned.1.call-start = ((), (), s32[]{:S(2)}) async-start(), calls=%async_computation.8 | async-start | bytes 1474560
  305.8 1.1 copy-start.1
  307.0 4.6 %collective-permute-start.1 = (bf16[16,32,640]{2,1,0:T(8,128)(2,1)S(1)}, bf16[16,32,640]{2,1,0:T(8,128)(2,1)}, u32[]{:S(2)}, u32[]{:S(2)}) collective-permute-start(bf16[16,32,640]{2,1,0:T(8,128)(2,1)S(1)} %convert_element_type.53), channel_id=1, source_target_pairs={{0,8},{8,0},{16,24},{24,16},{32,40},{40,32},{48,56},{56,48},{64,72... | collective-permute-start | bytes 1966088 | tf_op jit(solution)/shard_map/ppermute | solution.py:45
  313.5 20.4 %all-to-all-start.3 = ((bf16[16,16,640]{2,1,0:T(8,128)(2,1)}), bf16[16,16,640]{2,1,0:T(8,128)(2,1)S(1)}, u32[]{:S(2)}, u32[]{:S(2)}) async-start(bf16[16,16,640]{2,1,0:T(8,128)(2,1)} %fusion.20), calls=%async_computation.3 | async-start | bytes 655360 | tf_op jit(solution)/shard_map/all_to_all | solution.py:113
Sparse Core Ops, SparseCore 0:
  88.9 66.6 all-gather.7
  157.5 68.1 all-gather.3
  227.5 43.1 all-gather.5
  284.5 36.2 reduce-scatter.3
where the time goes:
time: 343 us
  waiting for transfers between devices  199 us (58%)
  blocking collectives  40.7 us (12%)
  matrix products  33.2 us (10%)
  starting transfers between devices  23.6 us (7%)
  local copies, waits for them, and re-layouts  23.2 us (7%)
  between operations  13.3 us (4%)
  other arithmetic  9.27 us (3%)
    all_gather x1, waiting for transfers between devices, on_device(): portion = lax.all_gather(received, 'tensor', axis=2, tiled=True)  63.9 us
    all_gather x1, waiting for transfers between devices, side_by_side(): lax.all_gather(both, axis, axis=dim, tiled=True)  41 us
    all_to_all x1, blocking collectives, on_device(): lax.all_to_all(to_send, 'dp', split_axis=0, concat_axis=0, tiled=True)  40.7 us
    all_gather x1, waiting for transfers between devices, on_device(): lax.all_gather(shared_down, 'dp', axis=1, tiled=True)  40.7 us
    all_to_all x1, waiting for transfers between devices, copy_for_each(): return lax.all_to_all(copies, axis, split_axis=0, concat_axis=0, tiled=True)  19.5 us
    all_to_all x1, waiting for transfers between devices, sum_at_owner(): lax.all_to_all(tiles, axis, split_axis=0, concat_axis=0, tiled=True)  17.9 us
    all_to_all x1, waiting for transfers between devices, on_device(): lax.all_to_all(kept_half, 'dp', split_axis=0, concat_axis=0, tiled=True)  11.9 us
    dot_general x1, matrix products, on_device(): jnp.dot(hidden_e, expert_down, preferred_element_type=jnp.float32)  11.2 us
  transfers between devices with their start and end apart: 9, of which 8 were waited for; matrix products, arithmetic and copies ran while one was open for 14% of the time, Pallas kernels for 0%

commit v1 on v0

--- a/solution.py
+++ b/solution.py
@@ -79,7 +79,9 @@
     shared_hidden = (jax.nn.silu(gate_sum) * up_sum).astype(jnp.bfloat16)
     shared_terms = jnp.dot(
         shared_hidden,
-        lax.all_gather(shared_down, "dp", axis=1, tiled=True),
+        jnp.concatenate(
+            lax.all_to_all(jnp.stack([shared_down] * lax.axis_size("dp")), "dp", 0, 0), axis=1
+        ),
         preferred_element_type=jnp.float32,
     )
     shared_out = lax.psum_scatter(

time: 343 us -> 414 us (1.21); the launches traced: 343 us -> 408 us
  waiting for transfers between devices: 199 us -> 263 us
    all_to_all x1, waiting for transfers between devices: 17.9 us -> 89.3 us  [sum_at_owner(): lax.all_to_all(tiles, axis, split_axis=0, concat_axis=0, tiled=True)]
    all_to_all x0 -> x1, waiting for transfers between devices: none -> 56.9 us  [on_device(): lax.all_to_all(jnp.stack([shared_down] * lax.axis_size('dp')), 'dp', 0, 0)]
    all_gather x1 -> x0, waiting for transfers between devices: 40.7 us -> none  [on_device(): lax.all_gather(shared_down, 'dp', axis=1, tiled=True)]
    all_gather x1, waiting for transfers between devices: 41 us -> 24 us  [side_by_side(): lax.all_gather(both, axis, axis=dim, tiled=True)]
    all_gather x1, waiting for transfers between devices: 63.9 us -> 57.1 us  [on_device(): portion = lax.all_gather(received, 'tensor', axis=2, tiled=True)]
    all_to_all x0 -> x1, starting transfers between devices: none -> 4.72 us  [on_device(): lax.all_to_all(jnp.stack([shared_down] * lax.axis_size('dp')), 'dp', 0, 0)]
    unnamed x16 -> x20, local copies, waits for them, and re-layouts: 9.48 us -> 8.51 us
  transfers between devices with their start and end apart: 9 -> 9, of which waited for: 8 -> 8; matrix products, arithmetic and copies ran while one was open for 14% -> 12% of each run, Pallas kernels for 0% -> 0%
where the time goes in v1:
time: 414 us; the launch traced here: 408 us
  waiting for transfers between devices  263 us (64%)
  blocking collectives  40.7 us (10%)
  matrix products  32.2 us (8%)
  starting transfers between devices  25.3 us (6%)
  local copies, waits for them, and re-layouts  25 us (6%)
  between operations  13.3 us (3%)
  other arithmetic  9.23 us (2%)
    all_to_all x1, waiting for transfers between devices, sum_at_owner(): lax.all_to_all(tiles, axis, split_axis=0, concat_axis=0, tiled=True)  89.3 us
    all_gather x1, waiting for transfers between devices, on_device(): portion = lax.all_gather(received, 'tensor', axis=2, tiled=True)  57.1 us
    all_to_all x1, waiting for transfers between devices, on_device(): lax.all_to_all(jnp.stack([shared_down] * lax.axis_size('dp')), 'dp', 0, 0)  56.9 us
    all_to_all x1, blocking collectives, on_device(): lax.all_to_all(to_send, 'dp', split_axis=0, concat_axis=0, tiled=True)  40.7 us
    all_gather x1, waiting for transfers between devices, side_by_side(): lax.all_gather(both, axis, axis=dim, tiled=True)  24 us
    all_to_all x1, waiting for transfers between devices, copy_for_each(): return lax.all_to_all(copies, axis, split_axis=0, concat_axis=0, tiled=True)  19.5 us
    all_to_all x1, waiting for transfers between devices, on_device(): lax.all_to_all(kept_half, 'dp', split_axis=0, concat_axis=0, tiled=True)  11.9 us
    dot_general x1, matrix products, on_device(): jnp.dot(hidden_e, expert_down, preferred_element_type=jnp.float32)  11.3 us
  transfers between devices with their start and end apart: 9, of which 8 were waited for; matrix products, arithmetic and copies ran while one was open for 12% of the time, Pallas kernels for 0%

profile of v1, /device:TPU:515, one launch (start us, length us, event | category | flops | bytes accessed | tf_op | source)
XLA Modules:
  0.0 408.3 jit_solution(3728576450878769849)
XLA Ops:
  6.6 1.2 copy.13
  7.8 1.3 broadcast_in_dim.8
  9.1 7.2 %all-to-all-start = ((bf16[8,128,640]{1,2,0:T(8,128)(2,1)}), bf16[8,128,640]{1,2,0:T(8,128)(2,1)}, u32[]{:S(2)}, u32[]{:S(2)}) async-start(bf16[8,128,640]{1,2,0:T(8,128)(2,1)} %broadcast_in_dim.8), calls=%async_computation | async-start | bytes 2621440 | tf_op jit(solution)/shard_map/all_to_all | solution.py:15
  16.2 19.5 %all-to-all-done = bf16[8,128,640]{1,2,0:T(8,128)(2,1)} async-done(((bf16[8,128,640]{1,2,0:T(8,128)(2,1)}), bf16[8,128,640]{1,2,0:T(8,128)(2,1)}, u32[]{:S(2)}, u32[]{:S(2)}) %all-to-all-start) | async-done | bytes 1310752 | tf_op jit(solution)/shard_map/all_to_all | solution.py:15
  35.7 1.6 fusion.17
  37.5 8.0 %scatter_fusion = bf16[8,32,640]{2,1,0:T(8,128)(2,1)S(1)} fusion(bf16[8,32,640]{2,1,0:T(8,128)(2,1)S(1)} %broadcast_in_dim.18, s32[128]{0:T(128)S(1)} %get-tuple-element.8, bf16[128,640]{1,0:T(8,128)(2,1)S(1)} %multiply_convert_fusion), kind=kCustom, calls=%fused_computation.1 | custom fusion | bytes 492544 | tf_op jit(solution)/shard_map/scatter | solution.py:74
  45.5 40.7 %all_to_all.25 = bf16[16,16,640]{2,1,0:T(8,128)(2,1)S(1)} all-to-all(bf16[16,16,640]{2,1,0:T(8,128)(2,1)S(1)} %bitcast.63), channel_id=1, replica_groups=mesh['group'=2,'dp'=16,'tensor'=8] {'dp'}, dimensions={0} | all-to-all | bytes 655360 | tf_op jit(solution)/shard_map/all_to_all | solution.py:92
  86.2 1.6 collective-permute-done
  87.9 0.9 pad_maximum_fusion.1
  88.9 2.0 pad_maximum_fusion
  91.0 2.8 stack.2
  93.8 4.7 %all-to-all-start.1 = ((bf16[16,512,320]{1,2,0:T(8,128)(2,1)}), bf16[16,512,320]{1,2,0:T(8,128)(2,1)}, u32[]{:S(2)}, u32[]{:S(2)}) async-start(bf16[16,512,320]{1,2,0:T(8,128)(2,1)} %stack.2), calls=%async_computation.1 | async-start | bytes 10485760 | tf_op jit(solution)/shard_map/all_to_all | solution.py:83
  98.6 57.1 %all-gather.5.cloned.1.call-done = bf16[16,32,5120]{2,1,0:T(8,128)(2,1)} async-done(((bf16[16,32,640]{2,1,0:T(8,128)(2,1)}), bf16[16,32,5120]{2,1,0:T(8,128)(2,1)}) %all-gather.5.cloned.1.call-update) | async-done | bytes 5242896 | tf_op jit(solution)/shard_map/all_gather | solution.py:102
  155.6 4.8 %fusion.40 = f32[512,256]{1,0:T(8,128)S(1)} fusion(bf16[512,5120]{1,0:T(8,128)(2,1)} %bitcast.68, bf16[5120,256]{1,0:T(8,128)(2,1)} %param.12), kind=kOutput, calls=%fused_computation.52 | convolution fusion | flops 1342177280 | bytes 8388608 | tf_op jit(solution)/shard_map/dot_general | solution.py:104
  160.5 11.3 %convolution_convert_fusion = bf16[512,5120]{1,0:T(8,128)(2,1)} fusion(bf16[256,5120]{1,0:T(8,128)(2,1)S(1)} %copy-done, bf16[512,5120]{1,0:T(8,128)(2,1)} %bitcast.69, bf16[5120,256]{1,0:T(8,128)(2,1)} %param.13, f32[512,256]{1,0:T(8,128)S(1)} %fusion.40), kind=kOutput, calls=%fused_computation.3 | convolution fusion | flops 2687762432 | bytes 16252928 | tf_op jit(solution)/shard_map/dot_general | solution.py:107
  171.8 3.7 copy.17
  175.4 3.0 copy.19
  178.5 56.9 %all-to-all-done.1 = bf16[16,512,320]{1,2,0:T(8,128)(2,1)} async-done(((bf16[16,512,320]{1,2,0:T(8,128)(2,1)}), bf16[16,512,320]{1,2,0:T(8,128)(2,1)}, u32[]{:S(2)}, u32[]{:S(2)}) %all-to-all-start.1) | async-done | bytes 5242912 | tf_op jit(solution)/shard_map/all_to_all | solution.py:83
  235.3 6.7 %all-to-all-start.3 = ((bf16[8,16,32,640]{3,2,1,0:T(8,128)(2,1)}), bf16[8,16,32,640]{3,2,1,0:T(8,128)(2,1)}, u32[]{:S(2)}, u32[]{:S(2)}) async-start(bf16[8,16,32,640]{3,2,1,0:T(8,128)(2,1)} %bitcast.61), calls=%async_computation.3 | async-start | bytes 10485760 | tf_op jit(solution)/shard_map/all_to_all | solution.py:38
  242.0 24.0 %all-gather.3.cloned.1.call-done = bf16[5120,1024]{1,0:T(8,128)(2,1)} async-done(((bf16[320,1024]{1,0:T(8,128)(2,1)}), bf16[5120,1024]{1,0:T(8,128)(2,1)}) %all-gather.3.cloned.1.call-update) | async-done | bytes 10485776 | tf_op jit(solution)/shard_map/all_gather | solution.py:24
  266.0 4.4 %fusion.5 = f32[128,512]{0,1:T(8,128)S(1)} fusion(bf16[128,5120]{0,1:T(8,128)(2,1)} %bitcast.1, bf16[5120,1024]{1,0:T(8,128)(2,1)} %all-gather.3.cloned.1.call-done), kind=kOutput, calls=%fused_computation.12 | convolution fusion | flops 671088640 | bytes 6815744 | tf_op jit(solution)/shard_map/dot_general | solution.py:77
  270.4 10.1 %convolution_convert_fusion.1 = bf16[128,5120]{1,0:T(8,128)(2,1)S(1)} fusion(bf16[512,5120]{0,1:T(8,128)(2,1)} %bitcast.6, bf16[128,5120]{0,1:T(8,128)(2,1)} %bitcast.1, bf16[5120,1024]{1,0:T(8,128)(2,1)} %all-gather.3.cloned.1.call-done, f32[128,512]{0,1:T(8,128)S(1)} %fusion.5), kind=kOutput, calls=%fused_computation.4 | convolution fusion | flops 1343225856 | bytes 13369344 | tf_op jit(solution)/shard_map/dot_general | solution.py:80
  280.6 1.5 copy.15
  282.1 89.3 %all-to-all-done.3 = bf16[8,16,32,640]{3,2,1,0:T(8,128)(2,1)} async-done(((bf16[8,16,32,640]{3,2,1,0:T(8,128)(2,1)}), bf16[8,16,32,640]{3,2,1,0:T(8,128)(2,1)}, u32[]{:S(2)}, u32[]{:S(2)}) %all-to-all-start.3) | async-done | bytes 5242912 | tf_op jit(solution)/shard_map/all_to_all | solution.py:38
  371.4 3.4 convert_reduce_fusion
  374.8 1.1 copy-done.2
  376.1 2.2 collective-permute-done.1
  378.3 2.0 fusion.20
  380.2 6.5 %all-to-all-start.4 = ((bf16[16,16,640]{2,1,0:T(8,128)(2,1)}), bf16[16,16,640]{2,1,0:T(8,128)(2,1)S(1)}, u32[]{:S(2)}, u32[]{:S(2)}) async-start(bf16[16,16,640]{2,1,0:T(8,128)(2,1)} %fusion.20), calls=%async_computation.4 | async-start | bytes 655360 | tf_op jit(solution)/shard_map/all_to_all | solution.py:115
  386.7 1.1 copy.16
  387.8 11.9 %all-to-all-done.4 = bf16[16,16,640]{2,1,0:T(8,128)(2,1)S(1)} async-done(((bf16[16,16,640]{2,1,0:T(8,128)(2,1)}), bf16[16,16,640]{2,1,0:T(8,128)(2,1)S(1)}, u32[]{:S(2)}, u32[]{:S(2)}) %all-to-all-start.4) | async-done | bytes 327712 | tf_op jit(solution)/shard_map/all_to_all | solution.py:115
  399.7 1.4 gather_fusion
  (31 shorter events, 1.4 us)
Async XLA Ops:
  6.5 153.9 %copy-start = (bf16[256,5120]{1,0:T(8,128)(2,1)S(1)}, bf16[256,5120]{1,0:T(8,128)(2,1)}, u32[]{:S(2)}) copy-start(bf16[256,5120]{1,0:T(8,128)(2,1)} %param.14) | copy-start | bytes 7864324
  6.6 9.7 %copy-start.7 = (s32[128]{0:T(128)S(1)}, s32[128]{0:T(128)}, u32[]{:S(2)}) copy-start(s32[128]{0:T(128)} %param.19) | copy-start | bytes 1540
  6.6 9.7 %copy-start.6 = (s32[128]{0:T(128)S(1)}, s32[128]{0:T(128)}, u32[]{:S(2)}) copy-start(s32[128]{0:T(128)} %param.18) | copy-start | bytes 1540
  6.6 29.2 %copy-start.5 = (bf16[5120,8]{0,1:T(8,128)(2,1)S(1)}, bf16[5120,8]{0,1:T(8,128)(2,1)}, u32[]{:S(2)}) copy-start(bf16[5120,8]{0,1:T(8,128)(2,1)} %param.11) | copy-start | bytes 245764
  7.8 29.6 %copy-start.3 = (bf16[128,640]{1,0:T(8,128)(2,1)S(1)}, bf16[128,640]{1,0:T(8,128)(2,1)}, u32[]{:S(2)}) copy-start(bf16[128,640]{1,0:T(8,128)(2,1)} %param.10) | copy-start | bytes 491524
  9.1 26.6 %all-to-all-start = ((bf16[8,128,640]{1,2,0:T(8,128)(2,1)}), bf16[8,128,640]{1,2,0:T(8,128)(2,1)}, u32[]{:S(2)}, u32[]{:S(2)}) async-start(bf16[8,128,640]{1,2,0:T(8,128)(2,1)} %broadcast_in_dim.8), calls=%async_computation | async-start | bytes 2621440 | tf_op jit(solution)/shard_map/all_to_all | solution.py:15
  16.2 139.4 %all-gather.5.cloned.1.call-start = ((), (), s32[]{:S(2)}) async-start(), calls=%async_computation.7 | async-start | bytes 5898240 | tf_op jit(solution)/shard_map/all_gather | solution.py:102
  86.2 1.6 collective-permute-start
  87.9 3.1 copy-start.4
  88.8 177.2 %all-gather.3.cloned.1.call-start = ((), (), s32[]{:S(2)}) async-start(), calls=%async_computation.6 | async-start | bytes 11141120 | tf_op jit(solution)/shard_map/all_gather | solution.py:24
  93.8 141.5 %all-to-all-start.1 = ((bf16[16,512,320]{1,2,0:T(8,128)(2,1)}), bf16[16,512,320]{1,2,0:T(8,128)(2,1)}, u32[]{:S(2)}, u32[]{:S(2)}) async-start(bf16[16,512,320]{1,2,0:T(8,128)(2,1)} %stack.2), calls=%async_computation.1 | async-start | bytes 10485760 | tf_op jit(solution)/shard_map/all_to_all | solution.py:83
  235.3 136.0 %all-to-all-start.3 = ((bf16[8,16,32,640]{3,2,1,0:T(8,128)(2,1)}), bf16[8,16,32,640]{3,2,1,0:T(8,128)(2,1)}, u32[]{:S(2)}, u32[]{:S(2)}) async-start(bf16[8,16,32,640]{3,2,1,0:T(8,128)(2,1)} %bitcast.61), calls=%async_computation.3 | async-start | bytes 10485760 | tf_op jit(solution)/shard_map/all_to_all | solution.py:38
  242.0 144.7 %reduce-scatter.4.cloned.1.call-start = ((), (), s32[]{:S(2)}) async-start(), calls=%async_computation.8 | async-start | bytes 1474560
  374.8 1.1 copy-start.2
  375.8 26.0 %copy-start.1 = (bf16[256,5120]{1,0:T(8,128)(2,1)S(1)}, bf16[256,5120]{1,0:T(8,128)(2,1)}, u32[]{:S(2)}) copy-start(bf16[256,5120]{1,0:T(8,128)(2,1)} %param.14) | copy-start | bytes 7864324
  375.9 2.4 collective-permute-start.1
  380.2 19.5 %all-to-all-start.4 = ((bf16[16,16,640]{2,1,0:T(8,128)(2,1)}), bf16[16,16,640]{2,1,0:T(8,128)(2,1)S(1)}, u32[]{:S(2)}, u32[]{:S(2)}) async-start(bf16[16,16,640]{2,1,0:T(8,128)(2,1)} %fusion.20), calls=%async_computation.4 | async-start | bytes 655360 | tf_op jit(solution)/shard_map/all_to_all | solution.py:115
Sparse Core Ops, SparseCore 0:
  89.0 66.6 all-gather.4
  157.5 108.4 all-gather.2
  282.2 64.0 reduce-scatter.3
